TPU v7x, 256 devices: a whole 4x4x8 slice. The times are simulated.
256 devices in a mesh: chan: 8 (over z_hi, x), clus: 32 (over z_lo, y, core).
Axes of the slice: x: 4, y: 4, z: 8 (z_hi: 2, z_lo: 4; z = z_hi * 4 + z_lo), core: 2. Of those that a mesh axis runs over, the one named last changes fastest.
Arguments:
- waveform: float32 [88, 1280], P('chan', 'clus'), may hold values from -33 to 33
- basis_slots: bfloat16 [88, 128, 8, 1024], P('chan', 'clus'), may hold values from -0.1875 to 0.1875
- slot_channel: int32 [88], P('chan'), may hold values from 0 to 87, as said below
- cluster_holder: int32 [64], replicated, may hold values from 0 to 31, as said below
- basis_count: int32 [64], replicated, may hold values from 1 to 8
Outputs:
- detection: float32 [64, 256], P('clus', 'chan')
Inputs may be any that keep to these rules, and one draw needn't show every extreme that they name: `slot_channel`: each aligned block of 11 entries holds the channel numbers of the same block, each once. `cluster_holder`: no index is named by more than 4 clusters and some index by exactly 4. Among the clusters c with the same c // 2, no index is named more than 2 times, and every index that is named is named exactly 2 times.
All inputs are finite; a program needn't handle non-finite values.
Results may differ from a plain program's by a relative error of at most 0.00045.
Values sent between devices are 32-bit elements; how exact they have to be, the bound alone decides.
A program may use at most 64 MiB of HBM per device.

v0:
```python
import jax
import jax.numpy as jnp
from jax import lax
from jax.experimental import pallas as pl
from jax.experimental.pallas import tpu as pltpu
from jax.sharding import PartitionSpec as P

MESH = pl.DeviceIdType.MESH

X, Z_HI, Z_LO, Y, CORE = 4, 2, 4, 4, 2
CLUS = Z_LO * Y * CORE
CHANS = 11
PIECE = 40
LANES = 128
LAGS = 256
WINDOW = 1024
RANK = 8
SLOTS = 4
CLUSTERS = 64
CHUNKS = 10
HANKELS = 9


def clus_steps():
    steps = [(dz, dy, dc) for dz in range(Z_LO) for dy in range(Y) for dc in range(CORE)]
    steps.remove((0, 0, 0))

    def distance(step):
        dz, dy, dc = step
        return (0, 2, 2, 2)[dz] + (0, 1, 2, 1)[dy] + 0.1 * dc

    return sorted(steps, key=distance, reverse=True)


def far_steps():
    steps = [(dh, *rest) for dh in range(Z_HI) for rest in [(0, 0, 0), *clus_steps()]]
    steps.remove((0, 0, 0, 0))

    def distance(step):
        dh, dz, dy, dc = step
        return 2 * dh + (0, 2, 2, 2)[dz] + (0, 1, 2, 1)[dy] + 0.1 * dc

    return sorted(steps, key=distance, reverse=True)


def kernel(
    wave_hbm, basis_hbm, slot_hbm, holder_hbm, count_hbm, out_ref,
    wave_v, basis_v, slot_s, holder_s, count_s,
    pieces, record, hankel, squares_v, tx_a, rx_a, tx_b, rx_b, tx_e, rx_e,
    load_sem, send_1, recv_1, send_a, recv_a, send_b, recv_b, send_e, recv_e,
):
    chan = lax.axis_index("chan")
    clus = lax.axis_index("clus")
    z_hi, x = chan // X, chan % X
    z_lo, y, core = clus // (Y * CORE), (clus // CORE) % Y, clus % CORE

    def clus_at(dz, dy, dc):
        return ((z_lo + dz) % Z_LO) * (Y * CORE) + ((y + dy) % Y) * CORE + (core + dc) % CORE

    def chan_at(dh, dx):
        return ((z_hi + dh) % Z_HI) * X + (x + dx) % X

    loads = [
        pltpu.make_async_copy(source, target, load_sem.at[n])
        for n, (source, target) in enumerate(
            [(wave_hbm, wave_v), (basis_hbm, basis_v), (slot_hbm, slot_s), (holder_hbm, holder_s), (count_hbm, count_s)]
        )
    ]
    loads[0].start()

    barrier = pltpu.get_barrier_semaphore()
    greeted = [(chan, clus_at(*step)) for step in clus_steps()]
    greeted += [(chan_at(0, dx), clus) for dx in (2, 1, 3)]
    greeted += [(chan_at(1, 0), clus)]
    for device in greeted:
        pl.semaphore_signal(barrier, inc=1, device_id=device, device_id_type=MESH)
    for load in loads[1:]:
        load.start()

    loads[0].wait()
    from_id = lax.broadcasted_iota(jnp.int32, (PIECE, PIECE), 0)
    to_id = lax.broadcasted_iota(jnp.int32, (PIECE, PIECE), 1)
    turn = jnp.where(from_id + to_id == PIECE - 1, 1.0, 0.0).astype(jnp.float32)
    turned = jnp.dot(wave_v[...], turn, precision=lax.Precision.HIGHEST, preferred_element_type=jnp.float32)
    pieces[clus] = jnp.zeros((4, LANES), jnp.float32)
    pieces[clus, :, 0:PIECE] = turned[0:4, :]
    pieces[clus, :, PIECE : 2 * PIECE] = turned[4:8, :]
    pieces[clus, 0:3, 2 * PIECE : 3 * PIECE] = turned[8:11, :]
    pl.semaphore_wait(barrier, len(greeted))

    for step in clus_steps():
        pltpu.make_async_remote_copy(
            src_ref=pieces.at[clus], dst_ref=pieces.at[clus], send_sem=send_1, recv_sem=recv_1,
            device_id=(chan, clus_at(*step)), device_id_type=MESH,
        ).start()

    for load in loads[1:]:
        load.wait()
    own = [2 * clus, 2 * clus + 1]
    own_holder = [holder_s[c] for c in own]

    def count_cluster(c, carry):
        held, ranks, positions = carry
        holder, rank = holder_s[c], count_s[c]
        mine = holder == clus
        ranks = tuple(
            r + jnp.where(jnp.logical_and(mine, held == p), rank, 0) for p, r in enumerate(ranks)
        )
        positions = tuple(
            n + jnp.where(jnp.logical_and(holder == h, c < o), 1, 0)
            for n, h, o in zip(positions, own_holder, own)
        )
        return held + jnp.where(mine, 1, 0), ranks, positions

    zero = jnp.int32(0)
    _, ranks, positions = lax.fori_loop(
        0, CLUSTERS, count_cluster, (zero, (zero,) * SLOTS, (zero,) * 2)
    )

    pltpu.make_async_copy(pieces.at[pl.ds(0, CLUS - 1)], pieces.at[pl.ds(0, CLUS - 1)], recv_1).wait()

    lane = lax.broadcasted_iota(jnp.int32, (4, LANES), 1)
    squares_v[...] = jnp.zeros((16, LANES), jnp.float32)
    for c in range(CHUNKS):
        rows = [jnp.zeros((4, LANES), jnp.float32)] * 3
        for i in range(CLUS):
            low = LANES * (c + 1) - PIECE * (i + 1)
            high = low + PIECE
            if high <= 0 or low >= LANES:
                continue
            inside = (lane >= low) & (lane < high)
            piece = pieces[i]
            for a in range(3):
                moved = pltpu.roll(piece, (low - PIECE * a) % LANES, 1)
                rows[a] = jnp.where(inside, moved, rows[a])
        for a in range(3):
            record[c, 4 * a : 4 * a + 4, :] = rows[a]
        total = jnp.sum(rows[0] * rows[0] + rows[1] * rows[1] + rows[2] * rows[2], axis=0, keepdims=True)
        squares_v[c : c + 1, :] = total

    squares = squares_v[...]
    row_id = lax.broadcasted_iota(jnp.int32, (LANES, LANES), 0)
    col_id = lax.broadcasted_iota(jnp.int32, (LANES, LANES), 1)
    upto = jnp.where(row_id <= col_id, 1.0, 0.0).astype(jnp.float32)
    prefix = jnp.dot(squares, upto, precision=lax.Precision.HIGHEST, preferred_element_type=jnp.float32)
    energy = []
    for h in range(2):
        whole = jnp.sum(prefix[h + 1 : h + 9, LANES - 1 : LANES], axis=0, keepdims=True)
        energy.append(prefix[h : h + 1, :] + (whole - prefix[h + 8 : h + 9, :]))

    near = row_id <= col_id
    captured = jnp.zeros((SLOTS * RANK, LAGS), jnp.float32)
    for j in range(CHANS):
        rolled = None
        for c in range(CHUNKS):
            later = pltpu.roll(
                jnp.broadcast_to(record[c, j : j + 1, :], (LANES, LANES)), 0, 1, stride=1, stride_axis=0
            )
            if c > 0:
                block = jnp.where(near, rolled, later)
                hankel[j, LANES * (c - 1) : LANES * c, :] = block.astype(jnp.bfloat16)
            rolled = later
        vectors = basis_v[lax.rem(slot_s[j], CHANS)]
        windows = jnp.concatenate([hankel[j, 0:WINDOW, :], hankel[j, LANES : LANES + WINDOW, :]], axis=1)
        projected = jnp.dot(vectors, windows, preferred_element_type=jnp.float32)
        captured = captured + projected * projected

    rank_id = lax.broadcasted_iota(jnp.int32, (RANK, LAGS), 0)
    tx_a[...] = jnp.zeros((X, 4, LANES), jnp.float32)
    for p in range(SLOTS):
        part = jnp.where(rank_id < ranks[p], captured[RANK * p : RANK * (p + 1), :], 0.0)
        row = jnp.sum(part, axis=0, keepdims=True)
        for h in range(2):
            for v in range(X):
                start = LANES * h + 32 * (X - 1 - v)
                tx_a[v, h : h + 1, 32 * p : 32 * (p + 1)] = row[:, start : start + 32]
    for h in range(2):
        for v in range(X):
            start = 32 * (X - 1 - v)
            tx_a[v, 2:3, 32 * h : 32 * (h + 1)] = energy[h][:, start : start + 32]

    for dx in (2, 1, 3):
        pltpu.make_async_remote_copy(
            src_ref=tx_a.at[(x + dx) % X], dst_ref=rx_a.at[x], send_sem=send_a, recv_sem=recv_a,
            device_id=(chan_at(0, dx), clus), device_id_type=MESH,
        ).start()
    rx_a[x] = tx_a[x]
    pltpu.make_async_copy(rx_a.at[pl.ds(0, X - 1)], rx_a.at[pl.ds(0, X - 1)], recv_a).wait()
    reduced = rx_a[0] + rx_a[1] + rx_a[2] + rx_a[3]

    tx_b[0] = reduced[0:1, :]
    tx_b[1] = reduced[1:2, :]
    tx_e[...] = reduced[2:3, :]
    me = z_hi * CLUS + clus
    energy_copy = pltpu.make_async_remote_copy(
        src_ref=tx_e, dst_ref=rx_e, send_sem=send_e, recv_sem=recv_e,
        device_id=(chan_at(1, 0), clus), device_id_type=MESH,
    )
    energy_copy.start()
    for dh, *step in far_steps():
        pltpu.make_async_remote_copy(
            src_ref=tx_b.at[(z_hi + dh) % Z_HI], dst_ref=rx_b.at[me], send_sem=send_b, recv_sem=recv_b,
            device_id=(chan_at(dh, 0), clus_at(*step)), device_id_type=MESH,
        ).start()
    rx_b[me] = tx_b[z_hi]
    energy_copy.wait_recv()
    both = reduced[2:3, :] + rx_e[...]
    energy_own = jnp.where(z_hi == 0, both[:, 0:32], both[:, 32:64]) + 1e-6
    pltpu.make_async_copy(rx_b.at[pl.ds(0, 2 * CLUS - 1)], rx_b.at[pl.ds(0, 2 * CLUS - 1)], recv_b).wait()
    for q in range(2):
        row = rx_b[own_holder[q]] + rx_b[CLUS + own_holder[q]]
        value = jnp.zeros((1, 32), jnp.float32)
        for p in range(SLOTS):
            value = jnp.where(positions[q] == p, row[:, 32 * p : 32 * (p + 1)], value)
        out_ref[q : q + 1, :] = (WINDOW / RANK) * value / energy_own

    pltpu.make_async_copy(pieces.at[pl.ds(0, CLUS - 1)], pieces.at[pl.ds(0, CLUS - 1)], send_1).wait()
    pltpu.make_async_copy(rx_a.at[pl.ds(0, X - 1)], rx_a.at[pl.ds(0, X - 1)], send_a).wait()
    pltpu.make_async_copy(rx_b.at[pl.ds(0, 2 * CLUS - 1)], rx_b.at[pl.ds(0, 2 * CLUS - 1)], send_b).wait()
    energy_copy.wait_send()


def local(waveform, basis_slots, slot_channel, cluster_holder, basis_count):
    basis = basis_slots.reshape(CHANS, SLOTS * RANK, WINDOW)
    f32 = jnp.float32
    latest_first = pl.pallas_call(
        kernel,
        out_shape=jax.ShapeDtypeStruct((2, 32), f32),
        in_specs=[pl.BlockSpec(memory_space=pltpu.HBM)] * 5,
        out_specs=pl.BlockSpec(memory_space=pltpu.VMEM),
        scratch_shapes=[
            pltpu.VMEM((CHANS, PIECE), f32),
            pltpu.VMEM((CHANS, SLOTS * RANK, WINDOW), jnp.bfloat16),
            pltpu.SMEM((CHANS,), jnp.int32),
            pltpu.SMEM((CLUSTERS,), jnp.int32),
            pltpu.SMEM((CLUSTERS,), jnp.int32),
            pltpu.VMEM((CLUS, 4, LANES), f32),
            pltpu.VMEM((CHUNKS, 16, LANES), f32),
            pltpu.VMEM((CHANS, HANKELS * LANES, LANES), jnp.bfloat16),
            pltpu.VMEM((16, LANES), f32),
            pltpu.VMEM((X, 4, LANES), f32),
            pltpu.VMEM((X, 4, LANES), f32),
            pltpu.VMEM((Z_HI, 1, LANES), f32),
            pltpu.VMEM((Z_HI * CLUS, 1, LANES), f32),
            pltpu.VMEM((1, LANES), f32),
            pltpu.VMEM((1, LANES), f32),
            pltpu.SemaphoreType.DMA((5,)),
            *[pltpu.SemaphoreType.DMA] * 8,
        ],
        compiler_params=pltpu.CompilerParams(collective_id=0, has_side_effects=True),
    )(waveform, basis, slot_channel, cluster_holder, basis_count)
    return latest_first[:, ::-1]


def solution(mesh):
    placed = (P("chan", "clus"), P("chan", "clus", None, None), P("chan"), P(), P())
    return jax.shard_map(
        local, mesh=mesh, in_specs=placed, out_specs=P("clus", "chan"), check_vma=False
    )
```

profile of v0, /device:TPU:1, one launch (start us, length us, event | category | flops | bytes accessed | tf_op | source)
XLA Modules:
  0.0 28.7 jit_solution(11327283483655342935)
XLA Ops:
  0.0 27.4 %shard_map.55 = f32[2,32]{1,0:T(2,128)} custom-call(f32[11,40]{1,0:T(8,128)} %wave_hbm.1, bf16[11,32,1024]{2,1,0:T(8,128)(2,1)} %bitcast.1, s32[11]{0:T(128)} %slot_hbm.1, s32[64]{0:T(128)} %holder_hbm.1, s32[64]{0:T(128)} %count_hbm.1), custom_call_target="tpu_custom_call" | custom-call | tf_op jit(solution)/shard_map/pallas_call | solution.py:226
  27.4 1.3 %rev.3 = f32[2,32]{1,0:T(2,128)} reverse(f32[2,32]{1,0:T(2,128)} %shard_map.55), dimensions={1} | reverse | bytes 512 | tf_op jit(solution)/shard_map/rev | solution.py:252
where the time goes:
time: 28.9 us; the launch traced here: 28.7 us
  Pallas kernels  27.4 us (95%)
  local copies, waits for them, and re-layouts  1.32 us (5%)
    pallas_call x1, Pallas kernels, local(): pl.pallas_call(kernel, out_shape=jax.ShapeDtypeStruct((2, 32), f32), in_s...  27.4 us
    rev x1, local copies, waits for them, and re-layouts, local(): return latest_first[:, ::-1]  1.32 us

commit v1 on v0

--- a/solution.py
+++ b/solution.py
@@ -32,15 +32,18 @@
     return sorted(steps, key=distance, reverse=True)
 
 
-def far_steps():
-    steps = [(dh, *rest) for dh in range(Z_HI) for rest in [(0, 0, 0), *clus_steps()]]
-    steps.remove((0, 0, 0, 0))
+def chip_steps():
+    steps = [(dh, dz, dy) for dh in range(Z_HI) for dz in range(Z_LO) for dy in range(Y)]
+    steps.remove((0, 0, 0))
 
     def distance(step):
-        dh, dz, dy, dc = step
-        return 2 * dh + (0, 2, 2, 2)[dz] + (0, 1, 2, 1)[dy] + 0.1 * dc
+        dh, dz, dy = step
+        return 2 * dh + (0, 2, 2, 2)[dz] + (0, 1, 2, 1)[dy]
 
     return sorted(steps, key=distance, reverse=True)
+
+
+X_STEPS = [(2, 1), (2, 0), (1, 1), (3, 1), (1, 0), (3, 0), (0, 1)]
 
 
 def kernel(
@@ -70,7 +73,7 @@
 
     barrier = pltpu.get_barrier_semaphore()
     greeted = [(chan, clus_at(*step)) for step in clus_steps()]
-    greeted += [(chan_at(0, dx), clus) for dx in (2, 1, 3)]
+    greeted += [(chan_at(0, dx), clus_at(0, 0, dc)) for dx, dc in X_STEPS if dx > 0]
     greeted += [(chan_at(1, 0), clus)]
     for device in greeted:
         pl.semaphore_signal(barrier, inc=1, device_id=device, device_id_type=MESH)
@@ -149,7 +152,8 @@
         energy.append(prefix[h : h + 1, :] + (whole - prefix[h + 8 : h + 9, :]))
 
     near = row_id <= col_id
-    captured = jnp.zeros((SLOTS * RANK, LAGS), jnp.float32)
+    none = jnp.zeros((SLOTS * RANK, LANES), jnp.bfloat16)
+    captured = jnp.zeros((2 * SLOTS * RANK, LANES), jnp.float32)
     for j in range(CHANS):
         rolled = None
         for c in range(CHUNKS):
@@ -161,52 +165,57 @@
                 hankel[j, LANES * (c - 1) : LANES * c, :] = block.astype(jnp.bfloat16)
             rolled = later
         vectors = basis_v[lax.rem(slot_s[j], CHANS)]
-        windows = jnp.concatenate([hankel[j, 0:WINDOW, :], hankel[j, LANES : LANES + WINDOW, :]], axis=1)
-        projected = jnp.dot(vectors, windows, preferred_element_type=jnp.float32)
+        halves = jnp.concatenate(
+            [jnp.concatenate([vectors, none], axis=1), jnp.concatenate([none, vectors], axis=1)], axis=0
+        )
+        projected = jnp.dot(halves, hankel[j], preferred_element_type=jnp.float32)
         captured = captured + projected * projected
 
-    rank_id = lax.broadcasted_iota(jnp.int32, (RANK, LAGS), 0)
+    rank_id = lax.broadcasted_iota(jnp.int32, (RANK, LANES), 0)
     tx_a[...] = jnp.zeros((X, 4, LANES), jnp.float32)
     for p in range(SLOTS):
-        part = jnp.where(rank_id < ranks[p], captured[RANK * p : RANK * (p + 1), :], 0.0)
-        row = jnp.sum(part, axis=0, keepdims=True)
         for h in range(2):
+            first = RANK * (SLOTS * h + p)
+            part = jnp.where(rank_id < ranks[p], captured[first : first + RANK, :], 0.0)
+            row = jnp.sum(part, axis=0, keepdims=True)
             for v in range(X):
-                start = LANES * h + 32 * (X - 1 - v)
+                start = 32 * (X - 1 - v)
                 tx_a[v, h : h + 1, 32 * p : 32 * (p + 1)] = row[:, start : start + 32]
     for h in range(2):
         for v in range(X):
             start = 32 * (X - 1 - v)
             tx_a[v, 2:3, 32 * h : 32 * (h + 1)] = energy[h][:, start : start + 32]
 
-    for dx in (2, 1, 3):
+    for dx, dc in X_STEPS:
         pltpu.make_async_remote_copy(
-            src_ref=tx_a.at[(x + dx) % X], dst_ref=rx_a.at[x], send_sem=send_a, recv_sem=recv_a,
-            device_id=(chan_at(0, dx), clus), device_id_type=MESH,
+            src_ref=tx_a.at[(x + dx) % X], dst_ref=rx_a.at[X * core + x], send_sem=send_a, recv_sem=recv_a,
+            device_id=(chan_at(0, dx), clus_at(0, 0, dc)), device_id_type=MESH,
         ).start()
-    rx_a[x] = tx_a[x]
-    pltpu.make_async_copy(rx_a.at[pl.ds(0, X - 1)], rx_a.at[pl.ds(0, X - 1)], recv_a).wait()
-    reduced = rx_a[0] + rx_a[1] + rx_a[2] + rx_a[3]
-
-    tx_b[0] = reduced[0:1, :]
-    tx_b[1] = reduced[1:2, :]
+    rx_a[X * core + x] = tx_a[x]
+    pltpu.make_async_copy(rx_a.at[pl.ds(0, len(X_STEPS))], rx_a.at[pl.ds(0, len(X_STEPS))], recv_a).wait()
+
+    for c in range(CORE):
+        first = X * c
+        reduced = (rx_a[first] + rx_a[first + 1]) + (rx_a[first + 2] + rx_a[first + 3])
+        for h in range(Z_HI):
+            tx_b[h, c] = reduced[h : h + 1, :]
     tx_e[...] = reduced[2:3, :]
-    me = z_hi * CLUS + clus
     energy_copy = pltpu.make_async_remote_copy(
         src_ref=tx_e, dst_ref=rx_e, send_sem=send_e, recv_sem=recv_e,
         device_id=(chan_at(1, 0), clus), device_id_type=MESH,
     )
     energy_copy.start()
-    for dh, *step in far_steps():
+    held_at = z_hi * CLUS + clus - core
+    for dh, dz, dy in chip_steps():
         pltpu.make_async_remote_copy(
-            src_ref=tx_b.at[(z_hi + dh) % Z_HI], dst_ref=rx_b.at[me], send_sem=send_b, recv_sem=recv_b,
-            device_id=(chan_at(dh, 0), clus_at(*step)), device_id_type=MESH,
+            src_ref=tx_b.at[(z_hi + dh) % Z_HI], dst_ref=rx_b.at[pl.ds(held_at, CORE)], send_sem=send_b, recv_sem=recv_b,
+            device_id=(chan_at(dh, 0), clus_at(dz, dy, 0)), device_id_type=MESH,
         ).start()
-    rx_b[me] = tx_b[z_hi]
+    rx_b[pl.ds(held_at, CORE)] = tx_b[z_hi]
     energy_copy.wait_recv()
     both = reduced[2:3, :] + rx_e[...]
     energy_own = jnp.where(z_hi == 0, both[:, 0:32], both[:, 32:64]) + 1e-6
-    pltpu.make_async_copy(rx_b.at[pl.ds(0, 2 * CLUS - 1)], rx_b.at[pl.ds(0, 2 * CLUS - 1)], recv_b).wait()
+    pltpu.make_async_copy(rx_b.at[pl.ds(0, Z_HI * CLUS - CORE)], rx_b.at[pl.ds(0, Z_HI * CLUS - CORE)], recv_b).wait()
     for q in range(2):
         row = rx_b[own_holder[q]] + rx_b[CLUS + own_holder[q]]
         value = jnp.zeros((1, 32), jnp.float32)
@@ -215,8 +224,8 @@
         out_ref[q : q + 1, :] = (WINDOW / RANK) * value / energy_own
 
     pltpu.make_async_copy(pieces.at[pl.ds(0, CLUS - 1)], pieces.at[pl.ds(0, CLUS - 1)], send_1).wait()
-    pltpu.make_async_copy(rx_a.at[pl.ds(0, X - 1)], rx_a.at[pl.ds(0, X - 1)], send_a).wait()
-    pltpu.make_async_copy(rx_b.at[pl.ds(0, 2 * CLUS - 1)], rx_b.at[pl.ds(0, 2 * CLUS - 1)], send_b).wait()
+    pltpu.make_async_copy(rx_a.at[pl.ds(0, len(X_STEPS))], rx_a.at[pl.ds(0, len(X_STEPS))], send_a).wait()
+    pltpu.make_async_copy(rx_b.at[pl.ds(0, Z_HI * CLUS - CORE)], rx_b.at[pl.ds(0, Z_HI * CLUS - CORE)], send_b).wait()
     energy_copy.wait_send()
 
 
@@ -239,16 +248,16 @@
             pltpu.VMEM((CHANS, HANKELS * LANES, LANES), jnp.bfloat16),
             pltpu.VMEM((16, LANES), f32),
             pltpu.VMEM((X, 4, LANES), f32),
-            pltpu.VMEM((X, 4, LANES), f32),
-            pltpu.VMEM((Z_HI, 1, LANES), f32),
+            pltpu.VMEM((CORE * X, 4, LANES), f32),
+            pltpu.VMEM((Z_HI, CORE, 1, LANES), f32),
             pltpu.VMEM((Z_HI * CLUS, 1, LANES), f32),
             pltpu.VMEM((1, LANES), f32),
             pltpu.VMEM((1, LANES), f32),
             pltpu.SemaphoreType.DMA((5,)),
             *[pltpu.SemaphoreType.DMA] * 8,
         ],
-        compiler_params=pltpu.CompilerParams(collective_id=0, has_side_effects=True),
-    )(waveform, basis, slot_channel, cluster_holder, basis_count)
+        compiler_params=pltpu.CompilerParams(collective_id=0, has_side_effects=True, vmem_limit_bytes=16<<20),
+    )(*[pltpu.with_memory_space_constraint(a, pltpu.HBM) for a in (waveform, basis, slot_channel, cluster_holder, basis_count)])
     return latest_first[:, ::-1]
 
 

time: 28.9 us -> 27.1 us (0.938)
  Pallas kernels: 27.4 us -> 26.3 us
  local copies, waits for them, and re-layouts: 1.32 us -> 0.65 us
    pallas_call x1, Pallas kernels: 27.4 us -> 26.3 us  [local(): pl.pallas_call(kernel, out_shape=jax.ShapeDtypeStruct((2, 32), f32), in_s...]
    rev x1, local copies, waits for them, and re-layouts: 1.32 us -> 0.65 us  [local(): return latest_first[:, ::-1]]
where the time goes in v1:
time: 27.1 us; the launch traced here: 27 us
  Pallas kernels  26.3 us (97%)
  local copies, waits for them, and re-layouts  0.65 us (2%)
    pallas_call x1, Pallas kernels, local(): pl.pallas_call(kernel, out_shape=jax.ShapeDtypeStruct((2, 32), f32), in_s...  26.3 us
    rev x1, local copies, waits for them, and re-layouts, local(): return latest_first[:, ::-1]  0.65 us

profile of v1, /device:TPU:1, one launch (start us, length us, event | category | flops | bytes accessed | tf_op | source)
XLA Modules:
  0.0 27.0 jit_solution(4569268442966329400)
XLA Ops:
  0.0 26.3 %shard_map.55 = f32[2,32]{1,0:T(2,128)S(1)} custom-call(f32[11,40]{1,0:T(8,128)} %wave_hbm.1, bf16[11,32,1024]{2,1,0:T(8,128)(2,1)} %bitcast.1, s32[11]{0:T(128)} %slot_hbm.1, s32[64]{0:T(128)} %holder_hbm.1, s32[64]{0:T(128)} %count_hbm.1), custom_call_target="tpu_custom_call" | custom-call | tf_op jit(solution)/shard_map/pallas_call | solution.py:235
  26.3 0.7 %rev.3 = f32[2,32]{1,0:T(2,128)} reverse(f32[2,32]{1,0:T(2,128)S(1)} %shard_map.55), dimensions={1} | reverse | bytes 512 | tf_op jit(solution)/shard_map/rev | solution.py:261
